TPU v7x, 32 devices: a whole 2x2x4 slice. The times are simulated.
32 devices in a mesh: blk: 2 (over y), uly: 4 (over x, core), dp: 4 (over z).
Axes of the slice: x: 2, y: 2, z: 4, core: 2. Of those that a mesh axis runs over, the one named last changes fastest.
Arguments:
- tokens: bfloat16 [1024, 4096], P(('uly', 'dp')), may hold values from -6 to 6
- expert_ids: int32 [1024, 8], P(('uly', 'dp')), may hold values from 0 to 15, all different within a row; in each aligned block of 64 rows (0 to 63, 64 to 127, ...) at most 40 rows name the same one
- route_weight: float32 [1024, 8], P(('uly', 'dp')), may hold values from 0.05 to 0.5
- w_gate: bfloat16 [16, 4096, 1024], P(('uly', 'dp'), None, 'blk'), may hold values from -0.09375 to 0.09375
- w_up: bfloat16 [16, 4096, 1024], P(('uly', 'dp'), None, 'blk'), may hold values from -0.09375 to 0.09375
- w_down: bfloat16 [16, 1024, 4096], P(('uly', 'dp'), 'blk'), may hold values from -0.1875 to 0.1875
Outputs:
- mixed: bfloat16 [1024, 4096], P(('uly', 'dp'), 'blk')
Inputs may be any that keep to these rules, and one draw needn't show every extreme that they name: `expert_ids`: each row names 8 different experts. In each aligned block of 64 rows (the rows of one device) no expert is named by more than 40 rows, and in some block one expert is named by exactly 40 rows.
All inputs are finite; a program needn't handle non-finite values.
Results may differ from a plain program's by a relative error of at most 0.015.
Values may be sent and summed in bfloat16 or wider, within the bound.
A program may use at most 64 MiB of HBM per device.

v0:
```python
import jax
import jax.numpy as jnp
from jax import lax
from jax.sharding import PartitionSpec as P


def routing_tables(expert_ids, route_weight, groups, local_count, capacity):
    tokens_here, picks_count = expert_ids.shape
    experts = groups * local_count
    labels = lax.broadcasted_iota(jnp.int32, (1, 1, experts), 2)
    onehot = (expert_ids[:, :, None] == labels).astype(jnp.int32)
    chosen = jnp.sum(onehot, axis=1)
    before = jnp.cumsum(chosen, axis=0) - chosen
    slot_of = jnp.sum(onehot * before[:, None, :], axis=2)
    places = lax.broadcasted_iota(jnp.int32, (1, 1, capacity), 2)
    slot_hot = (slot_of[:, :, None] == places).astype(jnp.float32)
    expert_hot = onehot.astype(jnp.float32).reshape(tokens_here, picks_count, groups, local_count)
    placing = jnp.einsum("tkgl,tkc->gclt", expert_hot, slot_hot)
    placing = placing.reshape(groups * capacity * local_count, tokens_here)
    mixing = jnp.einsum("tkgl,tkc,tk->tgcl", expert_hot, slot_hot, route_weight)
    mixing = mixing.reshape(tokens_here, groups * capacity * local_count)
    return (placing.astype(jnp.bfloat16), mixing)


def local_slots(tokens, expert_ids, route_weight, w_gate, w_up, w_down):
    ulysses_size = lax.axis_size("uly")
    data_size = lax.axis_size("dp")
    cycle_size = lax.axis_size("blk")
    tokens_here, model_width = tokens.shape
    local_count = w_gate.shape[0]
    hidden_cut = w_gate.shape[2]
    groups = ulysses_size * data_size
    experts = groups * local_count
    picks_count = expert_ids.shape[1]
    capacity = min(tokens_here, max(2, 5 * tokens_here * picks_count // (4 * experts)))
    placing, mixing = routing_tables(expert_ids, route_weight, groups, local_count, capacity)
    slice_width = model_width // cycle_size
    rows_total = groups * capacity
    cycle_index = lax.axis_index("blk")
    own_part = lax.dynamic_slice_in_dim(tokens, cycle_index * slice_width, slice_width, 1)
    outgoing = jnp.dot(placing, own_part, preferred_element_type=jnp.float32).astype(jnp.bfloat16)
    outgoing = outgoing.reshape(ulysses_size, data_size, capacity, local_count, slice_width)
    arrived = lax.all_to_all(
        lax.all_to_all(outgoing, "uly", split_axis=0, concat_axis=0, tiled=True),
        "dp",
        split_axis=1,
        concat_axis=1,
        tiled=True,
    )
    arrived = arrived.reshape(rows_total, local_count, slice_width)
    portion = lax.all_gather(arrived, "blk", axis=2, tiled=True)
    gate_more = jnp.einsum("rlw,lwf->rlf", portion, w_gate, preferred_element_type=jnp.float32)
    up_more = jnp.einsum("rlw,lwf->rlf", portion, w_up, preferred_element_type=jnp.float32)
    hidden = (jax.nn.silu(gate_more) * up_more).astype(jnp.bfloat16)
    resplit = lax.all_to_all(w_down, "blk", split_axis=2, concat_axis=1, tiled=True)
    zero_sum = jnp.zeros((slice_width, rows_total * local_count), jnp.float32)
    total = zero_sum
    portion = lax.all_gather(hidden, "blk", axis=2, tiled=True)
    ranges_count = portion.shape[2] // hidden_cut
    for number in range(ranges_count):
        part_hidden = portion[:, :, number * hidden_cut : (number + 1) * hidden_cut]
        part_rows = lax.dynamic_slice_in_dim(resplit, number * hidden_cut, hidden_cut, 1)
        partial_value = jnp.einsum(
            "lfd,rlf->drl", part_rows, part_hidden, preferred_element_type=jnp.float32
        )
        partial_value = partial_value.reshape(slice_width, rows_total * local_count)
        total = total + partial_value.astype(jnp.bfloat16).astype(jnp.float32)
    returned = total.astype(jnp.bfloat16).reshape(
        slice_width, ulysses_size, data_size, capacity, local_count
    )
    returned_rows = lax.all_to_all(
        lax.all_to_all(returned, "uly", split_axis=1, concat_axis=1, tiled=True),
        "dp",
        split_axis=2,
        concat_axis=2,
        tiled=True,
    )
    returned_rows = returned_rows.reshape(slice_width, rows_total * local_count).astype(jnp.float32)
    mixed = lax.dot_general(
        mixing, returned_rows, (((1,), (1,)), ((), ())), precision=lax.Precision.HIGHEST
    )
    return mixed.astype(jnp.bfloat16)


def local_dense(tokens, expert_ids, route_weight, w_gate, w_up, w_down):
    data_size = lax.axis_size("dp")
    local_count = w_gate.shape[0]
    groups = lax.axis_size("uly") * data_size
    experts = groups * local_count
    labels = lax.broadcasted_iota(jnp.int32, (1, 1, experts), 2)
    scaled = jnp.sum(
        jnp.where(expert_ids[:, :, None] == labels, route_weight[:, :, None], 0.0), axis=1
    )
    everyone = lax.all_gather(tokens, ("uly", "dp"), axis=0, tiled=True)
    shares = lax.all_gather(scaled, ("uly", "dp"), axis=0, tiled=True)
    first = (lax.axis_index("uly") * data_size + lax.axis_index("dp")) * local_count
    total = None
    for number in range(local_count):
        share = lax.dynamic_slice_in_dim(shares, first + number, 1, 1)
        gate = jnp.dot(everyone, w_gate[number], preferred_element_type=jnp.float32)
        up = jnp.dot(everyone, w_up[number], preferred_element_type=jnp.float32)
        hidden = (jax.nn.silu(gate) * up * share).astype(jnp.bfloat16)
        part = jnp.dot(hidden, w_down[number], preferred_element_type=jnp.float32)
        total = part if total is None else total + part
    halves = lax.psum_scatter(total.astype(jnp.bfloat16), "blk", scatter_dimension=1, tiled=True)
    return lax.psum_scatter(halves, ("uly", "dp"), scatter_dimension=0, tiled=True)


def solution(mesh):
    groups = mesh.shape["uly"] * mesh.shape["dp"]
    return jax.shard_map(
        local_dense if groups <= 16 else local_slots,
        mesh=mesh,
        in_specs=(
            P(("uly", "dp"), None),
            P(("uly", "dp"), None),
            P(("uly", "dp"), None),
            P(("uly", "dp"), None, "blk"),
            P(("uly", "dp"), None, "blk"),
            P(("uly", "dp"), "blk", None),
        ),
        out_specs=P(("uly", "dp"), "blk"),
        check_vma=False,
    )
```

profile of v0, /device:TPU:0, one launch (start us, length us, event | category | flops | bytes accessed | tf_op | source)
XLA Modules:
  0.0 293.6 jit_solution(17746111028157414352)
XLA Ops:
  6.5 0.0 all-gather.3.cloned.1.call-start
  6.5 0.7 all-gather.3.cloned.1.call-update
  7.3 0.0 reduce-scatter.3.cloned.1.call-start
  7.3 0.7 select_reduce_fusion
  8.0 36.9 %all-gather = f32[16,64,16]{1,2,0:T(8,128)S(1)} all-gather(f32[1,64,16]{1,2,0:T(8,128)S(1)} %bitcast.19), channel_id=1, replica_groups=mesh['blk'=2,'uly'=4,'dp'=4] {'uly','dp'}, dimensions={0}, use_global_device_ids=true | all-gather | bytes 69632 | tf_op jit(solution)/shard_map/all_gather | solution.py:95
  45.0 0.1 reshape.3
  45.1 43.0 %all-gather.3.cloned.1.call-done = bf16[1024,4096]{1,0:T(8,128)(2,1)} async-done(((bf16[64,4096]{1,0:T(8,128)(2,1)}), bf16[1024,4096]{1,0:T(8,128)(2,1)}) %all-gather.3.cloned.1.call-update) | async-done | bytes 8388624 | tf_op jit(solution)/shard_map/all_gather | solution.py:94
  88.2 8.1 %fusion.3 = f32[1024,512]{1,0:T(8,128)S(1)} fusion(bf16[1024,4096]{1,0:T(8,128)(2,1)} %all-gather.3.cloned.1.call-done, bf16[1,4096,512]{2,1,0:T(8,128)(2,1)} %param.9), kind=kOutput, calls=%fused_computation.4 | convolution fusion | flops 4294967296 | bytes 14680064 | tf_op jit(solution)/shard_map/dot_general | solution.py:100
  96.3 16.0 %convolution_convert_fusion = bf16[1024,4096]{1,0:T(8,128)(2,1)} fusion(bf16[1,512,4096]{2,1,0:T(8,128)(2,1)} %param.11, f32[1024,512]{1,0:T(8,128)S(1)} %fusion.3, bf16[1024,4096]{1,0:T(8,128)(2,1)} %all-gather.3.cloned.1.call-done, bf16[1,4096,512]{2,1,0:T(8,128)(2,1)} %param.10, f32[1024]{0:T(1024)S(1)} %bitcast.20), kind=kOutput, calls=%fused_computation | convolution fusion | flops 8597798912 | bytes 27267072 | tf_op jit(solution)/shard_map/dot_general | solution.py:103
  112.3 0.0 reduce-scatter.3.cloned.1.call-update
  112.3 0.0 reduce-scatter.5.cloned.1.call-start
  112.4 98.0 %reduce-scatter.3.cloned.1.call-done = bf16[1024,2048]{1,0:T(8,128)(2,1)} async-done(((bf16[1024,4096]{1,0:T(8,128)(2,1)}), bf16[1024,2048]{1,0:T(8,128)(2,1)}) %reduce-scatter.3.cloned.1.call-update) | async-done | bytes 4194320 | tf_op jit(solution)/shard_map/reduce_scatter | solution.py:105
  210.4 0.0 reduce-scatter.5.cloned.1.call-update
  210.4 76.7 %reduce-scatter.5.cloned.1.call-done = bf16[64,2048]{1,0:T(8,128)(2,1)} async-done(((bf16[1024,2048]{1,0:T(8,128)(2,1)}), bf16[64,2048]{1,0:T(8,128)(2,1)}) %reduce-scatter.5.cloned.1.call-update) | async-done | bytes 262160 | tf_op jit(solution)/shard_map/reduce_scatter | solution.py:106
  (2 shorter events, 0.1 us)
Async XLA Ops:
  6.5 81.6 %all-gather.3.cloned.1.call-start = ((), (), s32[]{:S(2)}) async-start(), calls=%async_computation.2 | async-start | bytes 8912896 | tf_op jit(solution)/shard_map/all_gather | solution.py:94
  7.3 203.1 %reduce-scatter.3.cloned.1.call-start = ((), (), s32[]{:S(2)}) async-start(), calls=%async_computation.3 | async-start | bytes 12582912 | tf_op jit(solution)/shard_map/reduce_scatter | solution.py:105
  112.3 174.8 %reduce-scatter.5.cloned.1.call-start = ((), (), s32[]{:S(2)}) async-start(), calls=%async_computation.4 | async-start | bytes 4456448 | tf_op jit(solution)/shard_map/reduce_scatter | solution.py:106
Sparse Core Ops, SparseCore 0:
  9.5 78.5 all-gather.2
  112.4 97.8 reduce-scatter.2
  214.2 72.7 reduce-scatter.4
where the time goes:
time: 294 us
  waiting for transfers between devices  218 us (74%)
  blocking collectives  36.9 us (13%)
  matrix products  24.1 us (8%)
  between operations  13.1 us (4%)
    reduce_scatter x1, waiting for transfers between devices, local_dense(): lax.psum_scatter(total.astype(jnp.bfloat16), 'blk', scatter_dimension=1,...  98 us
    reduce_scatter x1, waiting for transfers between devices, local_dense(): lax.psum_scatter(halves, ('uly', 'dp'), scatter_dimension=0, tiled=True)  76.7 us
    all_gather x1, waiting for transfers between devices, local_dense(): everyone = lax.all_gather(tokens, ('uly', 'dp'), axis=0, tiled=True)  43 us
    all_gather x1, blocking collectives, local_dense(): shares = lax.all_gather(scaled, ('uly', 'dp'), axis=0, tiled=True)  36.9 us
    dot_general x1, matrix products, local_dense(): part = jnp.dot(hidden, w_down[number], preferred_element_type=jnp.float32)  16 us
    dot_general x1, matrix products, local_dense(): gate = jnp.dot(everyone, w_gate[number], preferred_element_type=jnp.float32)  8.14 us
  transfers between devices with their start and end apart: 3, of which 3 were waited for; matrix products, arithmetic and copies ran while one was open for 0% of the time, Pallas kernels for 0%

commit v1 on v0

--- a/solution.py
+++ b/solution.py
@@ -2,6 +2,13 @@
 import jax.numpy as jnp
 from jax import lax
 from jax.sharding import PartitionSpec as P
+
+
+def serve_bands_by_axis(array_in, unit):
+    main = jnp.concatenate([array_in, unit], axis=1)
+    return jnp.split(
+        lax.all_gather(main, ("uly", "dp"), axis=0, tiled=True), [array_in.shape[1]], axis=1
+    )
 
 
 def routing_tables(expert_ids, route_weight, groups, local_count, capacity):
@@ -91,8 +98,7 @@
     scaled = jnp.sum(
         jnp.where(expert_ids[:, :, None] == labels, route_weight[:, :, None], 0.0), axis=1
     )
-    everyone = lax.all_gather(tokens, ("uly", "dp"), axis=0, tiled=True)
-    shares = lax.all_gather(scaled, ("uly", "dp"), axis=0, tiled=True)
+    everyone, shares = serve_bands_by_axis(tokens, scaled)
     first = (lax.axis_index("uly") * data_size + lax.axis_index("dp")) * local_count
     total = None
     for number in range(local_count):

time: 294 us -> 320 us (1.088)
  waiting for transfers between devices: 218 us -> 275 us
  blocking collectives: 36.9 us -> 0 us
    all_gather x1, waiting for transfers between devices: 43 us -> 99 us  [serve_bands_by_axis(): lax.all_gather(main, ('uly', 'dp'), axis=0, tiled=True)]
    all_gather x1 -> x0, blocking collectives: 36.9 us -> none  [local_dense(): shares = lax.all_gather(scaled, ('uly', 'dp'), axis=0, tiled=True)]
where the time goes in v1:
time: 320 us; the launch traced here: 319 us
  waiting for transfers between devices  275 us (86%)
  matrix products  26.5 us (8%)
  between operations  13.1 us (4%)
    reduce_scatter x1, waiting for transfers between devices, local_dense(): lax.psum_scatter(total.astype(jnp.bfloat16), 'blk', scatter_dimension=1,...  99.4 us
    all_gather x1, waiting for transfers between devices, serve_bands_by_axis(): lax.all_gather(main, ('uly', 'dp'), axis=0, tiled=True)  99 us
    reduce_scatter x1, waiting for transfers between devices, local_dense(): lax.psum_scatter(halves, ('uly', 'dp'), scatter_dimension=0, tiled=True)  76.7 us
    dot_general x1, matrix products, local_dense(): part = jnp.dot(hidden, w_down[number], preferred_element_type=jnp.float32)  17.1 us
    dot_general x1, matrix products, local_dense(): gate = jnp.dot(everyone, w_gate[number], preferred_element_type=jnp.float32)  9.31 us
  transfers between devices with their start and end apart: 3, of which 3 were waited for; matrix products, arithmetic and copies ran while one was open for 0% of the time, Pallas kernels for 0%

profile of v1, /device:TPU:0, one launch (start us, length us, event | category | flops | bytes accessed | tf_op | source)
XLA Modules:
  0.0 319.3 jit_solution(12720733927891132682)
XLA Ops:
  6.5 0.0 all-gather.2.cloned.1.call-start
  6.5 0.7 select_reduce_fusion
  7.3 0.1 copy.11
  7.3 1.1 convert_element_type.9
  8.5 1.1 pad_maximum_fusion
  9.5 0.0 all-gather.2.cloned.1.call-update
  9.5 0.0 reduce-scatter.3.cloned.1.call-start
  9.6 99.0 %all-gather.2.cloned.1.call-done = f32[1024,4112]{1,0:T(8,128)} async-done(((f32[64,4112]{1,0:T(8,128)}), f32[1024,4112]{1,0:T(8,128)}) %all-gather.2.cloned.1.call-update) | async-done | bytes 16842768 | tf_op jit(solution)/shard_map/all_gather | solution.py:10
  108.7 1.1 split.9
  109.7 0.4 dynamic-slice_reduce_fusion
  110.1 9.3 %fusion.2 = f32[1024,512]{1,0:T(8,128)S(1)} fusion(f32[1024,4112]{1,0:T(8,128)} %all-gather.2.cloned.1.call-done, bf16[1,4096,512]{2,1,0:T(8,128)(2,1)} %param.9), kind=kOutput, calls=%fused_computation.2 | convolution fusion | flops 4294967296 | bytes 14680064 | tf_op jit(solution)/shard_map/dot_general | solution.py:106
  119.4 17.1 %convolution_convert_fusion = bf16[1024,4096]{1,0:T(8,128)(2,1)} fusion(bf16[1,512,4096]{2,1,0:T(8,128)(2,1)} %param.11, f32[1024,512]{1,0:T(8,128)S(1)} %fusion.2, bf16[1,4096,512]{2,1,0:T(8,128)(2,1)} %param.10, f32[1024,4112]{1,0:T(8,128)} %all-gather.2.cloned.1.call-done, f32[1024]{0:T(1024)S(1)} %dynamic-slice_reduce_fusion), kind=kOutput, calls=%fused_computation.4 | convolution fusion | flops 8597798912 | bytes 27267072 | tf_op jit(solution)/shard_map/dot_general | solution.py:109
  136.6 0.0 reduce-scatter.3.cloned.1.call-update
  136.6 0.0 reduce-scatter.5.cloned.1.call-start
  136.6 99.4 %reduce-scatter.3.cloned.1.call-done = bf16[1024,2048]{1,0:T(8,128)(2,1)} async-done(((bf16[1024,4096]{1,0:T(8,128)(2,1)}), bf16[1024,2048]{1,0:T(8,128)(2,1)}) %reduce-scatter.3.cloned.1.call-update) | async-done | bytes 4194320 | tf_op jit(solution)/shard_map/reduce_scatter | solution.py:111
  236.1 0.0 reduce-scatter.5.cloned.1.call-update
  236.1 76.7 %reduce-scatter.5.cloned.1.call-done = bf16[64,2048]{1,0:T(8,128)(2,1)} async-done(((bf16[1024,2048]{1,0:T(8,128)(2,1)}), bf16[64,2048]{1,0:T(8,128)(2,1)}) %reduce-scatter.5.cloned.1.call-update) | async-done | bytes 262160 | tf_op jit(solution)/shard_map/reduce_scatter | solution.py:112
Async XLA Ops:
  6.5 102.1 %all-gather.2.cloned.1.call-start = ((), (), s32[]{:S(2)}) async-start(), calls=%async_computation.2 | async-start | bytes 18382848 | tf_op jit(solution)/shard_map/all_gather | solution.py:10
  9.5 226.5 %reduce-scatter.3.cloned.1.call-start = ((), (), s32[]{:S(2)}) async-start(), calls=%async_computation.3 | async-start | bytes 12582912 | tf_op jit(solution)/shard_map/reduce_scatter | solution.py:111
  136.6 176.2 %reduce-scatter.5.cloned.1.call-start = ((), (), s32[]{:S(2)}) async-start(), calls=%async_computation.4 | async-start | bytes 4456448 | tf_op jit(solution)/shard_map/reduce_scatter | solution.py:112
Sparse Core Ops, SparseCore 0:
  9.7 98.9 all-gather.1
  136.7 99.2 reduce-scatter.2
  239.9 72.7 reduce-scatter.4
